TPU v7x, 128 devices: a whole 4x4x4 slice. The times are simulated.
128 devices in a mesh: row: 64 (over y, x, z_hi, core), col: 2 (over z_lo).
Axes of the slice: x: 4, y: 4, z: 4 (z_hi: 2, z_lo: 2; z = z_hi * 2 + z_lo), core: 2. Of those that a mesh axis runs over, the one named last changes fastest.
Arguments:
- tokens: bfloat16 [1024, 8192], P('row', 'col'), may hold values from -6 to 6
- norm_gain: float32 [8192], P('col'), may hold values from 0.1 to 1.9
- gate_weight: bfloat16 [8192, 28672], P('col', 'row'), may hold values from -0.0625 to 0.0625
- up_weight: bfloat16 [8192, 28672], P('col', 'row'), may hold values from -0.0625 to 0.0625
- down_weight: bfloat16 [28672, 8192], P('row', 'col'), may hold values from -0.03125 to 0.03125
Outputs:
- mixed: bfloat16 [1024, 8192], P('row', 'col')
All inputs are finite; a program needn't handle non-finite values.
Results may differ from a plain program's by a relative error of at most 0.0065.
Values may be sent and summed in bfloat16 or wider, within the bound.
A program may use at most 128 MiB of HBM per device.

v0:
```python
import jax
import jax.numpy as jnp
from jax import lax
from jax.sharding import Mesh
from jax.sharding import PartitionSpec as P

D = 8192
ROW = ("row_0", "row_1", "row_2", "row_3")


def copy_for_each(x, axis):
    copies = jnp.broadcast_to(x, (lax.axis_size(axis), *x.shape))
    return lax.all_to_all(copies, axis, split_axis=0, concat_axis=0, tiled=True)


def taken_together(x, axis):
    everything = copy_for_each(x, axis)
    return jnp.sum(everything, axis=0)


def in_blocks(x, dim, count):
    before, after = (x.shape[:dim], x.shape[dim + 1 :])
    return jnp.moveaxis(x.reshape(*before, count, -1, *after), dim, 0)


def sum_at_owner(x, axis, dim):
    count = lax.axis_size(axis)
    blocks = lax.all_to_all(in_blocks(x, dim, count), axis, 0, 0, tiled=True)
    return jnp.sum(blocks, axis=0)


def in_order(blocks, dim):
    blocks = jnp.moveaxis(blocks, 0, dim)
    dims = blocks.shape
    return blocks.reshape(*dims[:dim], dims[dim] * dims[dim + 1], *dims[dim + 2 :])


def collect(x, axis, dim):
    blocks = copy_for_each(x, axis)
    return in_order(blocks, dim)


def summed_rows(x, chips, core, dim):
    sizes = (lax.axis_size(chips), lax.axis_size(core))
    blocks = in_blocks(x, dim, sizes[0] * sizes[1])
    inside = blocks.shape[1:]
    blocks = blocks.reshape(*sizes, *inside).swapaxes(0, 1).reshape(-1, *inside)
    blocks = lax.psum_scatter(blocks, core, scatter_dimension=0, tiled=True)
    return lax.psum_scatter(blocks, chips, scatter_dimension=0, tiled=True)[0]


def gated(both, width):
    return (jax.nn.silu(both[:, :width]) * both[:, width:]).astype(jnp.bfloat16)


def on_device(tokens, norm_gain, gate_weight, up_weight, down_weight):
    widened = tokens.astype(jnp.float32)
    squares = taken_together(jnp.sum(widened * widened, axis=1, keepdims=True), "col")
    normed = (widened * norm_gain[None, :] / jnp.sqrt(squares / D + 1e-05)).astype(jnp.bfloat16)
    width = gate_weight.shape[1]
    piece = lax.all_gather(normed, ROW, axis=0, tiled=True)
    gate_part = jnp.dot(piece, gate_weight, preferred_element_type=jnp.float32)
    up_part = jnp.dot(piece, up_weight, preferred_element_type=jnp.float32)
    partial_value = jnp.concatenate([gate_part, up_part], axis=1)
    shares = sum_at_owner(partial_value, "col", 0)
    hidden = collect(gated(shares, width), "col", 0)
    mixed = summed_rows(
        jnp.dot(hidden, down_weight, preferred_element_type=jnp.float32),
        ("row_0", "row_1", "row_2"),
        "row_3",
        0,
    )
    return mixed.astype(jnp.bfloat16)


def solution(mesh):
    finer = Mesh(
        mesh.devices.reshape(4, 4, 2, 2, mesh.shape["col"]),
        ("row_0", "row_1", "row_2", "row_3", "col"),
    )
    placed = (P(ROW, "col"), P("col"), P("col", ROW), P("col", ROW), P(ROW, "col"))
    return jax.shard_map(
        on_device, mesh=finer, in_specs=placed, out_specs=P(ROW, "col"), check_vma=False
    )
```

profile of v0, /device:TPU:0, one launch (start us, length us, event | category | flops | bytes accessed | tf_op | source)
XLA Modules:
  0.0 435.2 jit_solution(14296491897519222040)
XLA Ops:
  6.5 0.0 all-gather.2.cloned.1.call-start
  6.5 1.0 fusion.4
  7.6 6.9 %all_to_all.15 = f32[2,16,1]{1,2,0:T(1,128)S(1)} all-to-all(f32[2,16,1]{1,2,0:T(1,128)S(1)} %broadcast_in_dim.8), channel_id=1, replica_groups=mesh['row_0'=4,'row_1'=4,'row_2'=2,'row_3'=2,'col'=2] {'col'}, dimensions={0} | all-to-all | bytes 256 | tf_op jit(solution)/shard_map/all_to_all | solution.py:13
  14.5 1.7 fusion.3
  16.2 0.0 all-gather.2.cloned.1.call-update
  16.2 0.0 reduce-scatter.3.cloned.1.call-start
  16.2 85.4 %all-gather.2.cloned.1.call-done = bf16[1024,4096]{1,0:T(8,128)(2,1)} async-done(((bf16[16,4096]{1,0:T(8,128)(2,1)}), bf16[1024,4096]{1,0:T(8,128)(2,1)}) %all-gather.2.cloned.1.call-update) | async-done | bytes 8388624 | tf_op jit(solution)/shard_map/all_gather | solution.py:61
  101.6 0.0 copy-start
  101.6 0.0 copy-start.1
  101.6 7.7 %fusion.6 = f32[1024,448]{0,1:T(8,128)S(1)} fusion(bf16[1024,4096]{1,0:T(8,128)(2,1)} %all-gather.2.cloned.1.call-done, bf16[4096,448]{0,1:T(8,128)(2,1)} %param.8), kind=kOutput, calls=%fused_computation.14 | convolution fusion | flops 3758096384 | bytes 13893632 | tf_op jit(solution)/shard_map/dot_general | solution.py:63
  109.3 0.0 copy-done
  109.3 0.2 copy-done.1
  109.5 4.0 fusion.5
  113.5 0.5 pad_maximum_fusion
  114.0 0.5 copy.17
  114.5 46.0 %all_to_all.16 = f32[2,512,896]{1,2,0:T(8,128)} all-to-all(f32[2,512,896]{1,2,0:T(8,128)S(1)} %bitcast.22), channel_id=1, replica_groups=mesh['row_0'=4,'row_1'=4,'row_2'=2,'row_3'=2,'col'=2] {'col'}, dimensions={0} | all-to-all | bytes 7340032 | tf_op jit(solution)/shard_map/all_to_all | solution.py:28
  160.5 2.6 reduce_sum.29
  163.1 0.3 fusion.1
  163.4 0.1 broadcast_in_dim.9
  163.5 14.5 %all_to_all.17 = bf16[2,512,448]{1,2,0:T(8,128)(2,1)S(1)} all-to-all(bf16[2,512,448]{1,2,0:T(8,128)(2,1)S(1)} %broadcast_in_dim.9), channel_id=1, replica_groups=mesh['row_0'=4,'row_1'=4,'row_2'=2,'row_3'=2,'col'=2] {'col'}, dimensions={0} | all-to-all | bytes 1835008 | tf_op jit(solution)/shard_map/all_to_all | solution.py:13
  177.9 0.5 copy.9
  178.4 6.6 %convolution_bitcast_fusion = f32[2,32,16,4096]{3,2,0,1:T(8,128)S(1)} fusion(bf16[32,2,16,448]{3,2,1,0:T(8,128)(2,1)S(1)} %bitcast.23, bf16[448,4096]{1,0:T(8,128)(2,1)} %param.9), kind=kOutput, calls=%fused_computation | convolution fusion | flops 3758096384 | bytes 21364736 | tf_op jit(solution)/shard_map/dot_general | solution.py:68
  185.0 6.0 %copy.10 = f32[2,32,16,4096]{3,2,1,0:T(8,128)} copy(f32[2,32,16,4096]{3,2,0,1:T(8,128)S(1)} %convolution_bitcast_fusion) | data formatting | bytes 33554432 | tf_op jit(solution)/shard_map/transpose | solution.py:47
  191.0 0.0 reduce-scatter.3.cloned.1.call-update
  191.0 0.0 reduce-scatter.5.cloned.1.call-start
  191.1 24.7 %reduce-scatter.3.cloned.1.call-done = f32[32,16,4096]{2,1,0:T(8,128)} async-done(((f32[64,16,4096]{2,1,0:T(8,128)}), f32[32,16,4096]{2,1,0:T(8,128)}) %reduce-scatter.3.cloned.1.call-update) | async-done | bytes 8388624 | tf_op jit(solution)/shard_map/reduce_scatter | solution.py:48
  215.8 0.0 reduce-scatter.5.cloned.1.call-update
  215.8 211.3 %reduce-scatter.5.cloned.1.call-done = f32[1,16,4096]{2,1,0:T(8,128)} async-done(((f32[32,16,4096]{2,1,0:T(8,128)}), f32[1,16,4096]{2,1,0:T(8,128)}) %reduce-scatter.5.cloned.1.call-update) | async-done | bytes 262160 | tf_op jit(solution)/shard_map/reduce_scatter | solution.py:49
  427.0 1.6 convert_bitcast_fusion
  (3 shorter events, 0.0 us)
Async XLA Ops:
  6.5 95.1 %all-gather.2.cloned.1.call-start = ((), (), s32[]{:S(2)}) async-start(), calls=%async_computation.5 | async-start | bytes 8519680 | tf_op jit(solution)/shard_map/all_gather | solution.py:61
  16.2 199.6 %reduce-scatter.3.cloned.1.call-start = ((), (), s32[]{:S(2)}) async-start(), calls=%async_computation.6 | async-start | bytes 25165824 | tf_op jit(solution)/shard_map/reduce_scatter | solution.py:48
  101.6 7.7 %copy-start = (bf16[1024,4096]{1,0:T(8,128)(2,1)S(1)}, bf16[1024,4096]{1,0:T(8,128)(2,1)}, u32[]{:S(2)}) copy-start(bf16[1024,4096]{1,0:T(8,128)(2,1)} %all-gather.2.cloned.1.call-done) | copy-start | bytes 25165828
  101.6 7.9 %copy-start.1 = (bf16[4096,448]{0,1:T(8,128)(2,1)S(1)}, bf16[4096,448]{0,1:T(8,128)(2,1)}, u32[]{:S(2)}) copy-start(bf16[4096,448]{0,1:T(8,128)(2,1)} %param.7) | copy-start | bytes 11010052
  191.0 236.0 %reduce-scatter.5.cloned.1.call-start = ((), (), s32[]{:S(2)}) async-start(), calls=%async_computation.7 | async-start | bytes 8650752 | tf_op jit(solution)/shard_map/reduce_scatter | solution.py:49
Sparse Core Ops, SparseCore 0:
  16.3 85.2 all-gather.1
  191.2 24.5 reduce-scatter.2
  218.2 208.8 reduce-scatter.4
where the time goes:
time: 436 us; the launch traced here: 435 us
  waiting for transfers between devices  321 us (74%)
  blocking collectives  67.4 us (15%)
  matrix products  18.2 us (4%)
  between operations  13.2 us (3%)
  other arithmetic  7.72 us (2%)
  local copies, waits for them, and re-layouts  7.32 us (2%)
    reduce_scatter x1, waiting for transfers between devices, summed_rows(): return lax.psum_scatter(blocks, chips, scatter_dimension=0, tiled=True)[0]  211 us
    all_gather x1, waiting for transfers between devices, on_device(): piece = lax.all_gather(normed, ROW, axis=0, tiled=True)  85.4 us
    all_to_all x1, blocking collectives, sum_at_owner(): blocks = lax.all_to_all(in_blocks(x, dim, count), axis, 0, 0, tiled=True)  46 us
    reduce_scatter x1, waiting for transfers between devices, summed_rows(): blocks = lax.psum_scatter(blocks, core, scatter_dimension=0, tiled=True)  24.7 us
    all_to_all x2, blocking collectives, copy_for_each(): return lax.all_to_all(copies, axis, split_axis=0, concat_axis=0, tiled=True)  21.3 us
  transfers between devices with their start and end apart: 3, of which 3 were waited for; matrix products, arithmetic and copies ran while one was open for 0% of the time, Pallas kernels for 0%

commit v1 on v0

--- a/solution.py
+++ b/solution.py
@@ -58,7 +58,9 @@
     squares = taken_together(jnp.sum(widened * widened, axis=1, keepdims=True), "col")
     normed = (widened * norm_gain[None, :] / jnp.sqrt(squares / D + 1e-05)).astype(jnp.bfloat16)
     width = gate_weight.shape[1]
-    piece = lax.all_gather(normed, ROW, axis=0, tiled=True)
+    piece = jnp.concatenate(
+        lax.all_to_all(jnp.stack([normed] * lax.axis_size(ROW)), ROW, 0, 0), axis=0
+    )
     gate_part = jnp.dot(piece, gate_weight, preferred_element_type=jnp.float32)
     up_part = jnp.dot(piece, up_weight, preferred_element_type=jnp.float32)
     partial_value = jnp.concatenate([gate_part, up_part], axis=1)

time: 436 us -> 456 us (1.046)
  blocking collectives: 67.4 us -> 176 us
  waiting for transfers between devices: 321 us -> 236 us
    all_to_all x0 -> x1, blocking collectives: none -> 109 us  [on_device(): lax.all_to_all(jnp.stack([normed] * lax.axis_size(ROW)), ROW, 0, 0)]
    all_gather x1 -> x0, waiting for transfers between devices: 85.4 us -> none  [on_device(): piece = lax.all_gather(normed, ROW, axis=0, tiled=True)]
  transfers between devices with their start and end apart: 3 -> 2, of which waited for: 3 -> 2; matrix products, arithmetic and copies ran while one was open for 0% -> 0% of each run, Pallas kernels for 0% -> 0%
where the time goes in v1:
time: 456 us; the launch traced here: 455 us
  waiting for transfers between devices  236 us (52%)
  blocking collectives  176 us (39%)
  matrix products  14.5 us (3%)
  between operations  13.5 us (3%)
  local copies, waits for them, and re-layouts  8.11 us (2%)
  other arithmetic  7.06 us (2%)
    reduce_scatter x1, waiting for transfers between devices, summed_rows(): return lax.psum_scatter(blocks, chips, scatter_dimension=0, tiled=True)[0]  211 us
    all_to_all x1, blocking collectives, on_device(): lax.all_to_all(jnp.stack([normed] * lax.axis_size(ROW)), ROW, 0, 0)  109 us
    all_to_all x1, blocking collectives, sum_at_owner(): blocks = lax.all_to_all(in_blocks(x, dim, count), axis, 0, 0, tiled=True)  46 us
    reduce_scatter x1, waiting for transfers between devices, summed_rows(): blocks = lax.psum_scatter(blocks, core, scatter_dimension=0, tiled=True)  24.4 us
    all_to_all x2, blocking collectives, copy_for_each(): return lax.all_to_all(copies, axis, split_axis=0, concat_axis=0, tiled=True)  21.3 us
  transfers between devices with their start and end apart: 2, of which 2 were waited for; matrix products, arithmetic and copies ran while one was open for 0% of the time, Pallas kernels for 0%

profile of v1, /device:TPU:0, one launch (start us, length us, event | category | flops | bytes accessed | tf_op | source)
XLA Modules:
  0.0 455.2 jit_solution(8718932914547556747)
XLA Ops:
  6.5 0.0 reduce-scatter.3.cloned.1.call-start
  6.5 1.0 fusion.4
  7.6 6.9 %all_to_all.20 = f32[2,16,1]{1,2,0:T(1,128)S(1)} all-to-all(f32[2,16,1]{1,2,0:T(1,128)S(1)} %broadcast_in_dim.8), channel_id=1, replica_groups=mesh['row_0'=4,'row_1'=4,'row_2'=2,'row_3'=2,'col'=2] {'col'}, dimensions={0} | all-to-all | bytes 256 | tf_op jit(solution)/shard_map/all_to_all | solution.py:13
  14.5 1.0 fusion.3
  15.5 1.0 stack.2
  16.5 0.0 copy-start
  16.6 108.7 %all_to_all.21 = bf16[64,16,4096]{2,1,0:T(8,128)(2,1)S(1)} all-to-all(bf16[64,16,4096]{2,1,0:T(8,128)(2,1)S(1)} %stack.2), channel_id=1, replica_groups=mesh['row_0'=4,'row_1'=4,'row_2'=2,'row_3'=2,'col'=2] {'row_0','row_1','..., dimensions={0} | all-to-all | bytes 16777216 | tf_op jit(solution)/shard_map/all_to_all | solution.py:62
  125.3 0.0 copy-done
  125.3 0.0 copy-start.1
  125.3 4.0 fusion.6
  129.3 0.0 copy-done.1
  129.3 4.0 fusion.5
  133.3 0.5 pad_maximum_fusion
  133.8 0.5 copy.17
  134.2 46.0 %all_to_all.22 = f32[2,512,896]{1,2,0:T(8,128)} all-to-all(f32[2,512,896]{1,2,0:T(8,128)S(1)} %bitcast.23), channel_id=1, replica_groups=mesh['row_0'=4,'row_1'=4,'row_2'=2,'row_3'=2,'col'=2] {'col'}, dimensions={0} | all-to-all | bytes 7340032 | tf_op jit(solution)/shard_map/all_to_all | solution.py:28
  180.3 2.6 reduce_sum.29
  182.9 0.3 fusion.1
  183.2 0.1 broadcast_in_dim.9
  183.2 14.4 %all_to_all.23 = bf16[2,512,448]{1,2,0:T(8,128)(2,1)S(1)} all-to-all(bf16[2,512,448]{1,2,0:T(8,128)(2,1)S(1)} %broadcast_in_dim.9), channel_id=1, replica_groups=mesh['row_0'=4,'row_1'=4,'row_2'=2,'row_3'=2,'col'=2] {'col'}, dimensions={0} | all-to-all | bytes 1835008 | tf_op jit(solution)/shard_map/all_to_all | solution.py:13
  197.7 0.5 copy.9
  198.2 6.6 %convolution_bitcast_fusion = f32[2,32,16,4096]{3,2,0,1:T(8,128)S(1)} fusion(bf16[32,2,16,448]{3,2,1,0:T(8,128)(2,1)S(1)} %bitcast.26, bf16[448,4096]{1,0:T(8,128)(2,1)} %param.9), kind=kOutput, calls=%fused_computation | convolution fusion | flops 3758096384 | bytes 21364736 | tf_op jit(solution)/shard_map/dot_general | solution.py:70
  204.8 6.0 %copy.10 = f32[2,32,16,4096]{3,2,1,0:T(8,128)} copy(f32[2,32,16,4096]{3,2,0,1:T(8,128)S(1)} %convolution_bitcast_fusion) | data formatting | bytes 33554432 | tf_op jit(solution)/shard_map/transpose | solution.py:47
  210.8 0.0 reduce-scatter.3.cloned.1.call-update
  210.8 0.0 reduce-scatter.5.cloned.1.call-start
  210.9 24.4 %reduce-scatter.3.cloned.1.call-done = f32[32,16,4096]{2,1,0:T(8,128)} async-done(((f32[64,16,4096]{2,1,0:T(8,128)}), f32[32,16,4096]{2,1,0:T(8,128)}) %reduce-scatter.3.cloned.1.call-update) | async-done | bytes 8388624 | tf_op jit(solution)/shard_map/reduce_scatter | solution.py:48
  235.2 0.0 reduce-scatter.5.cloned.1.call-update
  235.2 211.4 %reduce-scatter.5.cloned.1.call-done = f32[1,16,4096]{2,1,0:T(8,128)} async-done(((f32[32,16,4096]{2,1,0:T(8,128)}), f32[1,16,4096]{2,1,0:T(8,128)}) %reduce-scatter.5.cloned.1.call-update) | async-done | bytes 262160 | tf_op jit(solution)/shard_map/reduce_scatter | solution.py:49
  446.7 1.6 convert_bitcast_fusion
  (3 shorter events, 0.0 us)
Async XLA Ops:
  6.5 228.7 %reduce-scatter.3.cloned.1.call-start = ((), (), s32[]{:S(2)}) async-start(), calls=%async_computation.6 | async-start | bytes 25165824 | tf_op jit(solution)/shard_map/reduce_scatter | solution.py:48
  16.5 108.8 %copy-start = (bf16[4096,448]{0,1:T(8,128)(2,1)S(1)}, bf16[4096,448]{0,1:T(8,128)(2,1)}, u32[]{:S(2)}) copy-start(bf16[4096,448]{0,1:T(8,128)(2,1)} %param.8) | copy-start | bytes 11010052
  125.3 4.0 copy-start.1
  210.8 235.9 %reduce-scatter.5.cloned.1.call-start = ((), (), s32[]{:S(2)}) async-start(), calls=%async_computation.7 | async-start | bytes 8650752 | tf_op jit(solution)/shard_map/reduce_scatter | solution.py:49
Sparse Core Ops, SparseCore 0:
  210.9 24.2 reduce-scatter.2
  237.6 209.0 reduce-scatter.4
